TPU v7x, 32 devices: a whole 2x2x4 slice. The times are simulated.
32 devices in a mesh: seq: 4 (over y, x), tp: 8 (over z, core).
Axes of the slice: x: 2, y: 2, z: 4, core: 2. Of those that a mesh axis runs over, the one named last changes fastest.
Arguments:
- tokens: bfloat16 [1024, 4096], P('seq', 'tp'), may hold values from -30 to 30
- w_qkv: bfloat16 [4096, 3, 2048], P('seq', None, 'tp'), may hold values from -1 to 1
- keep_list: int32 [512], P('seq'), may hold values from 0 to 255, as said below
- counts: int32 [4], P('seq'), may hold values from 1 to 127, as said below
Outputs:
- attended: bfloat16 [256, 2048], P('seq', 'tp')
Inputs may be any that keep to these rules, and one draw needn't show every extreme that they name: `counts`: the entries sum to 256; one shard keeps 2 * 64 - 1 tokens and one shard keeps 1. `keep_list`: entries s * 2 * 64 to s * 2 * 64 + 2 * 64 - 1 are distinct token indices within shard s; the first counts[s] of them increase.
All inputs are finite; a program needn't handle non-finite values.
Results may differ from a plain program's by a relative error of at most 0.0065.
Values may be sent and summed in bfloat16 or wider, within the bound.
No kernel may reach another device: no remote copies, remote signals or barrier semaphores. Data moves between devices by JAX's collectives and lax.ppermute only.
A program may use at most 64 MiB of HBM per device.

v0:
```python
import jax
import jax.numpy as jnp
from jax import lax
from jax.sharding import PartitionSpec as P

HD = 128


def entering(value, axis, join, neutral):
    count, mine = (lax.axis_size(axis), lax.axis_index(axis))
    pieces = lax.all_gather(value, axis)
    so_far = jnp.full_like(value, 0) + jnp.asarray(neutral, value.dtype)

    def lap(position, so_far):
        longer = join(so_far, pieces[position])
        return jnp.where(position < mine, longer, so_far)

    return lax.fori_loop(0, count - 1, lap, so_far)


def add_sums(earlier, later):
    return earlier + later


def on_device(tokens, w_qkv, keep_list, counts):
    shards = lax.axis_size("seq")
    my_index = lax.axis_index("seq")
    tok_dev = tokens.shape[0]
    slots = keep_list.shape[0]
    capacity = slots // 2
    per_peer = slots // shards
    head_dim = HD
    columns = w_qkv.shape[2]
    local_heads = columns // head_dim
    offset = entering(counts, "seq", add_sums, jnp.zeros_like(counts))[0]
    peers = jnp.arange(shards, dtype=jnp.int32)[:, None]
    rounds = jnp.arange(per_peer, dtype=jnp.int32)[None, :]
    local_slot = (peers - offset) % shards + rounds * shards
    live = local_slot < counts[0]
    token_index = keep_list[local_slot]
    ranks = jnp.where(live, offset + local_slot, -1).astype(jnp.int32)
    positions = my_index * tok_dev + token_index
    meta = jnp.stack([positions, ranks], axis=2)
    picked = jnp.where(live[:, :, None], tokens[token_index], jnp.zeros((), tokens.dtype))
    arrived, arrived_meta = (
        lax.all_to_all(picked, "seq", split_axis=0, concat_axis=0, tiled=True),
        lax.all_to_all(meta, "seq", split_axis=0, concat_axis=0, tiled=True),
    )
    arrived_meta = arrived_meta.reshape(shards * per_peer, 2)
    arrived_rank = arrived_meta[:, 1]
    target = jnp.where(arrived_rank >= 0, arrived_rank // shards, capacity)
    flat = arrived.reshape(shards * per_peer, arrived.shape[2])
    kept = jnp.zeros((capacity, flat.shape[1]), flat.dtype).at[target].set(flat, mode="drop")
    kept_pos = jnp.zeros((capacity,), jnp.int32).at[target].set(arrived_meta[:, 0], mode="drop")
    full_rows = lax.all_gather(kept, "tp", axis=1, tiled=True)
    piece = lax.all_gather(w_qkv, "seq", axis=0, tiled=True)
    part_rows = lax.slice_in_dim(full_rows, 0, piece.shape[0], axis=1)
    projected = jnp.einsum(
        "rd,dgc->rgc", part_rows, piece, preferred_element_type=jnp.float32
    ).astype(jnp.bfloat16)
    queries = projected[:, 0].reshape(capacity, local_heads, head_dim)
    key_values = projected[:, 1:]
    scale = head_dim ** (-0.5)
    all_kv, all_pos = (
        lax.all_gather(key_values, "seq", axis=0, tiled=True),
        lax.all_gather(kept_pos, "seq", axis=0, tiled=True),
    )
    total_keys = all_kv.shape[0]
    keys_all = all_kv[:, 0].reshape(total_keys, local_heads, head_dim)
    values_all = all_kv[:, 1].reshape(total_keys, local_heads, head_dim)
    scores = (
        jnp.einsum("qhd,khd->hqk", queries, keys_all, preferred_element_type=jnp.float32) * scale
    )
    masked = all_pos[None, None, :] > kept_pos[None, :, None]
    scores = jnp.where(masked, -jnp.inf, scores)
    top = jnp.max(scores, axis=2, keepdims=True)
    expo = jnp.exp(scores - top)
    numer = jnp.einsum(
        "hqk,khd->hqd", expo.astype(jnp.bfloat16), values_all, preferred_element_type=jnp.float32
    )
    result = numer / jnp.sum(expo, axis=2)[..., None]
    return jnp.transpose(result, (1, 0, 2)).reshape(capacity, columns).astype(jnp.bfloat16)


def solution(mesh):
    in_specs = (P("seq", "tp"), P("seq", None, "tp"), P("seq"), P("seq"))
    out_specs = P("seq", "tp")
    return jax.shard_map(
        on_device, mesh=mesh, in_specs=in_specs, out_specs=out_specs, check_vma=False
    )
```

profile of v0, /device:TPU:0, one launch (start us, length us, event | category | flops | bytes accessed | tf_op | source)
XLA Modules:
  0.0 104.7 jit_solution(6532559039854450984)
XLA Ops:
  6.5 0.0 copy-start
  6.5 0.0 all-gather.3.cloned.1.call-start
  6.5 0.7 all-gather.3.cloned.1.call-update
  7.9 1.2 %dynamic-slice = u32[1]{0:T(128)} dynamic-slice(u32[32]{0:T(128)} %constant.83, u32[]{:T(128)S(6)} %add.147), dynamic_slice_sizes={1} | dynamic-slice | bytes 12
  9.1 0.7 dynamic-update-slice
  9.8 8.8 %all-reduce = s32[4]{0:T(128)S(1)} all-reduce(s32[4]{0:T(128)S(1)} %dynamic-update-slice), channel_id=2, replica_groups=mesh['seq'=4,'tp'=8] {'seq'}, use_global_device_ids=true, to_apply=%add | all-reduce | flops 4 | bytes 32
  18.6 3.5 %while.13 = (s32[]{:T(128)}, s32[1]{0:T(128)}, s32[]{:T(128)}, s32[4,1]{0,1:T(1,128)S(1)}, s32[]{:T(128)}) while((s32[]{:T(128)}, s32[1]{0:T(128)}, s32[]{:T(128)}, s32[4,1]{0,1:T(1,128)S(1)}, s32[]{:T(128)}) %tuple.38), condition=%wide.region_1.2_spmd, body=%wide.region_0.1_spmd.sunk | while | flops 5 | bytes 115 | solution.py:18
  18.6 0.6 constant_dynamic-slice_fusion.2
  19.8 0.6 constant_dynamic-slice_fusion.2
  21.0 0.6 constant_dynamic-slice_fusion.2
  22.2 0.1 compare_select_fusion.1
  22.2 0.1 reshape.223
  22.3 1.6 %gather_fusion = s32[128]{0:T(128)S(1)} fusion(s32[128]{0:T(128)} %param.8, s32[1024]{0:T(1024)S(1)} %pad_clamp_fusion.1), kind=kCustom, calls=%fused_computation | custom fusion | bytes 1536 | tf_op jit(solution)/shard_map/gather | solution.py:40
  23.9 0.1 gather.9
  24.0 0.6 copy.17
  24.6 3.2 %all-to-all-start = ((s32[4,32,2]{1,2,0:T(2,128)}), s32[4,32,2]{1,2,0:T(2,128)S(1)}, u32[]{:S(2)}, u32[]{:S(2)}) async-start(s32[4,32,2]{1,2,0:T(2,128)} %copy.17), calls=%async_computation | async-start | bytes 8192 | tf_op jit(solution)/shard_map/all_to_all | solution.py:47
  27.9 0.1 reshape.231
  28.0 0.0 copy-done
  28.0 0.8 gather_fusion.1
  28.8 0.1 add_compare_fusion.1
  28.9 0.7 broadcast_select_fusion
  30.2 2.5 %all-to-all-done = s32[4,32,2]{1,2,0:T(2,128)S(1)} async-done(((s32[4,32,2]{1,2,0:T(2,128)}), s32[4,32,2]{1,2,0:T(2,128)S(1)}, u32[]{:S(2)}, u32[]{:S(2)}) %all-to-all-start) | async-done | bytes 1056 | tf_op jit(solution)/shard_map/all_to_all | solution.py:47
  32.7 3.3 %all-to-all-start.1 = ((bf16[4,32,512]{2,1,0:T(8,128)(2,1)}), bf16[4,32,512]{2,1,0:T(8,128)(2,1)S(1)}, u32[]{:S(2)}, u32[]{:S(2)}) async-start(bf16[4,32,512]{2,1,0:T(8,128)(2,1)} %broadcast_select_fusion), calls=%async_computation.1 | async-start | bytes 262144 | tf_op jit(solution)/shard_map/all_to_all | solution.py:46
  36.0 0.1 reshape.219
  36.1 1.0 scatter_custom_fusion
  37.1 0.2 dynamic-update-slice.1
  37.4 7.8 %all-reduce.1 = s32[256]{0:T(256)S(1)} all-reduce(s32[256]{0:T(256)S(1)} %dynamic-update-slice.1), channel_id=1, replica_groups=mesh['seq'=4,'tp'=8] {'seq'}, use_global_device_ids=true, to_apply=%add.1 | all-reduce | flops 256 | bytes 2048
  45.2 0.1 broadcast_compare_fusion
  45.3 0.0 all-to-all-done.1
  45.3 1.1 %scatter_custom_fusion.1 = bf16[64,512]{1,0:T(8,128)(2,1)S(1)} fusion(s32[128]{0:T(128)S(1)} %get-tuple-element.98, bf16[128,512]{1,0:T(8,128)(2,1)S(1)} %bitcast.50, bf16[]{:T(256)} %constant.77.clone.1), kind=kCustom, calls=%fused_computation.22 | custom fusion | bytes 65538 | tf_op jit(solution)/shard_map/scatter | solution.py:53
  46.4 15.2 %all_gather.21 = bf16[64,4096]{1,0:T(8,128)(2,1)S(1)} all-gather(bf16[64,512]{1,0:T(8,128)(2,1)S(1)} %scatter_custom_fusion.1), channel_id=1, replica_groups=mesh['seq'=4,'tp'=8] {'tp'}, dimensions={1}, use_global_device_ids=true | all-gather | bytes 589824 | tf_op jit(solution)/shard_map/all_gather | solution.py:55
  61.6 21.9 %all-gather.3.cloned.1.call-done = bf16[4096,3,256]{2,0,1:T(8,128)(2,1)} async-done(((bf16[1024,3,256]{2,0,1:T(8,128)(2,1)}), bf16[4096,3,256]{2,0,1:T(8,128)(2,1)}) %all-gather.3.cloned.1.call-update) | async-done | bytes 6291472 | tf_op jit(solution)/shard_map/all_gather | solution.py:56
  83.5 4.0 %convolution_convert_fusion = bf16[64,3,256]{2,0,1:T(8,128)(2,1)S(1)} fusion(bf16[4096,3,256]{2,0,1:T(8,128)(2,1)} %all-gather.3.cloned.1.call-done, bf16[64,4096]{1,0:T(8,128)(2,1)S(1)} %all_gather.21), kind=kOutput, calls=%fused_computation.5 | convolution fusion | flops 402702336 | bytes 6914048 | tf_op jit(solution)/shard_map/rd,dgc->rgc/dot_general | solution.py:58
  87.5 9.0 %all_gather.23 = bf16[256,2,256]{2,0,1:T(8,128)(2,1)S(1)} all-gather(bf16[64,2,256]{2,0,1:T(8,128)(2,1)S(1)} %slice.29), channel_id=1, replica_groups=mesh['seq'=4,'tp'=8] {'seq'}, dimensions={0}, use_global_device_ids=true | all-gather | bytes 327680 | tf_op jit(solution)/shard_map/all_gather | solution.py:65
  96.6 0.3 fusion.20
  96.8 0.2 fusion.7
  97.0 0.2 fusion.3
  97.2 0.6 copy.35
  (16 shorter events, 0.2 us)
Async XLA Ops:
  6.5 21.5 %copy-start = (bf16[256,512]{1,0:T(8,128)(2,1)S(1)}, bf16[256,512]{1,0:T(8,128)(2,1)}, u32[]{:S(2)}) copy-start(bf16[256,512]{1,0:T(8,128)(2,1)} %param.6) | copy-start | bytes 786436
  6.5 76.9 %all-gather.3.cloned.1.call-start = ((), (), s32[]{:S(2)}) async-start(), calls=%async_computation.2 | async-start | bytes 7864320 | tf_op jit(solution)/shard_map/all_gather | solution.py:56
  24.6 8.0 %all-to-all-start = ((s32[4,32,2]{1,2,0:T(2,128)}), s32[4,32,2]{1,2,0:T(2,128)S(1)}, u32[]{:S(2)}, u32[]{:S(2)}) async-start(s32[4,32,2]{1,2,0:T(2,128)} %copy.17), calls=%async_computation | async-start | bytes 8192 | tf_op jit(solution)/shard_map/all_to_all | solution.py:47
  32.7 12.6 %all-to-all-start.1 = ((bf16[4,32,512]{2,1,0:T(8,128)(2,1)}), bf16[4,32,512]{2,1,0:T(8,128)(2,1)S(1)}, u32[]{:S(2)}, u32[]{:S(2)}) async-start(bf16[4,32,512]{2,1,0:T(8,128)(2,1)} %broadcast_select_fusion), calls=%async_computation.1 | async-start | bytes 262144 | tf_op jit(solution)/shard_map/all_to_all | solution.py:46
Sparse Core Ops, SparseCore 0:
  9.2 74.2 all-gather.2
where the time goes:
time: 105 us
  blocking collectives  40.9 us (39%)
  waiting for transfers between devices  25 us (24%)
  between operations  14.7 us (14%)
  local copies, waits for them, and re-layouts  10 us (10%)
  starting transfers between devices  6.57 us (6%)
  matrix products  4.44 us (4%)
  loops' own time  1.78 us (2%)
  other arithmetic  1.21 us (1%)
    all_gather x1, waiting for transfers between devices, on_device(): piece = lax.all_gather(w_qkv, 'seq', axis=0, tiled=True)  21.9 us
    unnamed x2, blocking collectives  16.7 us
    all_gather x1, blocking collectives, on_device(): full_rows = lax.all_gather(kept, 'tp', axis=1, tiled=True)  15.2 us
    all_gather x1, blocking collectives, on_device(): lax.all_gather(key_values, 'seq', axis=0, tiled=True)  9.02 us
    dot_general x1, matrix products, on_device(): jnp.einsum('rd,dgc->rgc', part_rows, piece, preferred_element_type=jnp.fl...  3.97 us
    all_to_all x1, starting transfers between devices, on_device(): lax.all_to_all(picked, 'seq', split_axis=0, concat_axis=0, tiled=True)  3.32 us
    all_to_all x1, starting transfers between devices, on_device(): lax.all_to_all(meta, 'seq', split_axis=0, concat_axis=0, tiled=True)  3.25 us
    all_to_all x1, waiting for transfers between devices, on_device(): lax.all_to_all(meta, 'seq', split_axis=0, concat_axis=0, tiled=True)  2.48 us
  transfers between devices with their start and end apart: 3, of which 2 were waited for; matrix products, arithmetic and copies ran while one was open for 10% of the time, Pallas kernels for 0%

commit v1 on v0

--- a/solution.py
+++ b/solution.py
@@ -52,7 +52,7 @@
     flat = arrived.reshape(shards * per_peer, arrived.shape[2])
     kept = jnp.zeros((capacity, flat.shape[1]), flat.dtype).at[target].set(flat, mode="drop")
     kept_pos = jnp.zeros((capacity,), jnp.int32).at[target].set(arrived_meta[:, 0], mode="drop")
-    full_rows = lax.all_gather(kept, "tp", axis=1, tiled=True)
+    full_rows = jnp.concatenate(lax.all_gather(kept, "tp"), axis=1)
     piece = lax.all_gather(w_qkv, "seq", axis=0, tiled=True)
     part_rows = lax.slice_in_dim(full_rows, 0, piece.shape[0], axis=1)
     projected = jnp.einsum(

time: 105 us -> 105 us (level)
  no operation moved by 1% of the time
where the time goes in v1:
time: 105 us
  blocking collectives  40.9 us (39%)
  waiting for transfers between devices  24.5 us (23%)
  between operations  14.7 us (14%)
  local copies, waits for them, and re-layouts  10.5 us (10%)
  starting transfers between devices  6.57 us (6%)
  matrix products  4.44 us (4%)
  loops' own time  1.78 us (2%)
  other arithmetic  1.21 us (1%)
    all_gather x1, waiting for transfers between devices, on_device(): piece = lax.all_gather(w_qkv, 'seq', axis=0, tiled=True)  21.3 us
    unnamed x2, blocking collectives  16.7 us
    all_gather x1, blocking collectives, on_device(): full_rows = jnp.concatenate(lax.all_gather(kept, 'tp'), axis=1)  15.2 us
    all_gather x1, blocking collectives, on_device(): lax.all_gather(key_values, 'seq', axis=0, tiled=True)  9.02 us
    dot_general x1, matrix products, on_device(): jnp.einsum('rd,dgc->rgc', part_rows, piece, preferred_element_type=jnp.fl...  3.97 us
    all_to_all x1, starting transfers between devices, on_device(): lax.all_to_all(picked, 'seq', split_axis=0, concat_axis=0, tiled=True)  3.32 us
    all_to_all x1, starting transfers between devices, on_device(): lax.all_to_all(meta, 'seq', split_axis=0, concat_axis=0, tiled=True)  3.25 us
    all_to_all x1, waiting for transfers between devices, on_device(): lax.all_to_all(meta, 'seq', split_axis=0, concat_axis=0, tiled=True)  2.48 us
  transfers between devices with their start and end apart: 3, of which 2 were waited for; matrix products, arithmetic and copies ran while one was open for 10% of the time, Pallas kernels for 0%

profile of v1, /device:TPU:0, one launch (start us, length us, event | category | flops | bytes accessed | tf_op | source)
XLA Modules:
  0.0 104.7 jit_solution(2758272804027856466)
XLA Ops:
  6.5 0.0 copy-start
  6.5 0.0 all-gather.4.cloned.1.call-start
  6.5 0.7 all-gather.4.cloned.1.call-update
  7.9 1.2 %dynamic-slice = u32[1]{0:T(128)} dynamic-slice(u32[32]{0:T(128)} %constant.83, u32[]{:T(128)S(6)} %add.147), dynamic_slice_sizes={1} | dynamic-slice | bytes 12
  9.1 0.7 dynamic-update-slice
  9.8 8.8 %all-reduce = s32[4]{0:T(128)S(1)} all-reduce(s32[4]{0:T(128)S(1)} %dynamic-update-slice), channel_id=2, replica_groups=mesh['seq'=4,'tp'=8] {'seq'}, use_global_device_ids=true, to_apply=%add | all-reduce | flops 4 | bytes 32
  18.6 3.5 %while.13 = (s32[]{:T(128)}, s32[1]{0:T(128)}, s32[]{:T(128)}, s32[4,1]{0,1:T(1,128)S(1)}, s32[]{:T(128)}) while((s32[]{:T(128)}, s32[1]{0:T(128)}, s32[]{:T(128)}, s32[4,1]{0,1:T(1,128)S(1)}, s32[]{:T(128)}) %tuple.38), condition=%wide.region_1.2_spmd, body=%wide.region_0.1_spmd.sunk | while | flops 5 | bytes 115 | solution.py:18
  18.6 0.6 constant_dynamic-slice_fusion.2
  19.8 0.6 constant_dynamic-slice_fusion.2
  21.0 0.6 constant_dynamic-slice_fusion.2
  22.2 0.1 compare_select_fusion.1
  22.2 0.1 reshape.231
  22.3 1.6 %gather_fusion = s32[128]{0:T(128)S(1)} fusion(s32[128]{0:T(128)} %param.8, s32[1024]{0:T(1024)S(1)} %pad_clamp_fusion.1), kind=kCustom, calls=%fused_computation | custom fusion | bytes 1536 | tf_op jit(solution)/shard_map/gather | solution.py:40
  23.9 0.1 gather.9
  24.0 0.6 copy.19
  24.6 3.2 %all-to-all-start = ((s32[4,32,2]{1,2,0:T(2,128)}), s32[4,32,2]{1,2,0:T(2,128)S(1)}, u32[]{:S(2)}, u32[]{:S(2)}) async-start(s32[4,32,2]{1,2,0:T(2,128)} %copy.19), calls=%async_computation | async-start | bytes 8192 | tf_op jit(solution)/shard_map/all_to_all | solution.py:47
  27.9 0.1 reshape.239
  28.0 0.0 copy-done
  28.0 0.8 gather_fusion.1
  28.8 0.1 add_compare_fusion.1
  28.9 0.7 broadcast_select_fusion
  30.2 2.5 %all-to-all-done = s32[4,32,2]{1,2,0:T(2,128)S(1)} async-done(((s32[4,32,2]{1,2,0:T(2,128)}), s32[4,32,2]{1,2,0:T(2,128)S(1)}, u32[]{:S(2)}, u32[]{:S(2)}) %all-to-all-start) | async-done | bytes 1056 | tf_op jit(solution)/shard_map/all_to_all | solution.py:47
  32.7 3.3 %all-to-all-start.1 = ((bf16[4,32,512]{2,1,0:T(8,128)(2,1)}), bf16[4,32,512]{2,1,0:T(8,128)(2,1)S(1)}, u32[]{:S(2)}, u32[]{:S(2)}) async-start(bf16[4,32,512]{2,1,0:T(8,128)(2,1)} %broadcast_select_fusion), calls=%async_computation.1 | async-start | bytes 262144 | tf_op jit(solution)/shard_map/all_to_all | solution.py:46
  36.0 0.1 reshape.225
  36.1 1.0 scatter_custom_fusion
  37.1 0.2 dynamic-update-slice.1
  37.4 7.8 %all-reduce.1 = s32[256]{0:T(256)S(1)} all-reduce(s32[256]{0:T(256)S(1)} %dynamic-update-slice.1), channel_id=1, replica_groups=mesh['seq'=4,'tp'=8] {'seq'}, use_global_device_ids=true, to_apply=%add.1 | all-reduce | flops 256 | bytes 2048
  45.2 0.1 broadcast_compare_fusion
  45.3 0.0 all-to-all-done.1
  45.3 1.1 %scatter_custom_fusion.1 = bf16[64,512]{1,0:T(8,128)(2,1)S(1)} fusion(s32[128]{0:T(128)S(1)} %get-tuple-element.98, bf16[128,512]{1,0:T(8,128)(2,1)S(1)} %bitcast.52, bf16[]{:T(256)} %constant.77.clone.1), kind=kCustom, calls=%fused_computation.21 | custom fusion | bytes 65538 | tf_op jit(solution)/shard_map/scatter | solution.py:53
  46.4 15.2 %all-gather.1 = bf16[512,512]{1,0:T(8,128)(2,1)S(1)} all-gather(bf16[64,512]{1,0:T(8,128)(2,1)S(1)} %scatter_custom_fusion.1), channel_id=3, replica_groups=mesh['seq'=4,'tp'=8] {'tp'}, dimensions={0}, use_global_device_ids=true | all-gather | bytes 589824 | tf_op jit(solution)/shard_map/all_gather | solution.py:55
  61.6 0.3 copy.21
  61.9 0.2 reshape.276
  62.1 21.3 %all-gather.4.cloned.1.call-done = bf16[4096,3,256]{2,0,1:T(8,128)(2,1)} async-done(((bf16[1024,3,256]{2,0,1:T(8,128)(2,1)}), bf16[4096,3,256]{2,0,1:T(8,128)(2,1)}) %all-gather.4.cloned.1.call-update) | async-done | bytes 6291472 | tf_op jit(solution)/shard_map/all_gather | solution.py:56
  83.5 4.0 %convolution_convert_fusion = bf16[64,3,256]{2,0,1:T(8,128)(2,1)S(1)} fusion(bf16[64,4096,1]{1,0,2:T(8,128)(2,1)S(1)} %reshape.276, bf16[4096,3,256]{2,0,1:T(8,128)(2,1)} %all-gather.4.cloned.1.call-done), kind=kOutput, calls=%fused_computation.5 | convolution fusion | flops 402702336 | bytes 6914048 | tf_op jit(solution)/shard_map/rd,dgc->rgc/dot_general | solution.py:58
  87.5 9.0 %all_gather.27 = bf16[256,2,256]{2,0,1:T(8,128)(2,1)S(1)} all-gather(bf16[64,2,256]{2,0,1:T(8,128)(2,1)S(1)} %slice.29), channel_id=1, replica_groups=mesh['seq'=4,'tp'=8] {'seq'}, dimensions={0}, use_global_device_ids=true | all-gather | bytes 327680 | tf_op jit(solution)/shard_map/all_gather | solution.py:65
  96.6 0.3 fusion.19
  96.8 0.2 fusion.6
  97.0 0.2 fusion.3
  97.2 0.6 copy.38
  (16 shorter events, 0.2 us)
Async XLA Ops:
  6.5 21.5 %copy-start = (bf16[256,512]{1,0:T(8,128)(2,1)S(1)}, bf16[256,512]{1,0:T(8,128)(2,1)}, u32[]{:S(2)}) copy-start(bf16[256,512]{1,0:T(8,128)(2,1)} %param.6) | copy-start | bytes 786436
  6.5 76.9 %all-gather.4.cloned.1.call-start = ((), (), s32[]{:S(2)}) async-start(), calls=%async_computation.2 | async-start | bytes 7864320 | tf_op jit(solution)/shard_map/all_gather | solution.py:56
  24.6 8.0 %all-to-all-start = ((s32[4,32,2]{1,2,0:T(2,128)}), s32[4,32,2]{1,2,0:T(2,128)S(1)}, u32[]{:S(2)}, u32[]{:S(2)}) async-start(s32[4,32,2]{1,2,0:T(2,128)} %copy.19), calls=%async_computation | async-start | bytes 8192 | tf_op jit(solution)/shard_map/all_to_all | solution.py:47
  32.7 12.6 %all-to-all-start.1 = ((bf16[4,32,512]{2,1,0:T(8,128)(2,1)}), bf16[4,32,512]{2,1,0:T(8,128)(2,1)S(1)}, u32[]{:S(2)}, u32[]{:S(2)}) async-start(bf16[4,32,512]{2,1,0:T(8,128)(2,1)} %broadcast_select_fusion), calls=%async_computation.1 | async-start | bytes 262144 | tf_op jit(solution)/shard_map/all_to_all | solution.py:46
Sparse Core Ops, SparseCore 0:
  9.2 74.2 all-gather.3
